TPU v7x, 32 devices: a whole 2x2x4 slice. The times are simulated.
32 devices in a mesh: grp: 2 (over core), tile: 16 (over z, y, x).
Axes of the slice: x: 2, y: 2, z: 4, core: 2. Of those that a mesh axis runs over, the one named last changes fastest.
Arguments:
- source_points: float32 [2, 3, 524288], P('grp', None, 'tile'), may hold values from -6 to 6
- intersection: int32 [2, 2048, 1], P('grp', 'tile'), may hold values from 0 to 15; in each aligned block of 128 rows (0 to 127, 128 to 255, ..., all dimensions but the last counted through in order) at most 16 rows name the same one
- target_scan: int32 [2, 2048], P('grp', 'tile'), may hold values from 0 to 63
- matches: int32 [2, 524288], P('grp', 'tile'), may hold values from 0 to 511
- target_points: float32 [3, 524288], P(None, 'tile'), may hold values from -6 to 6
- target_normals: float32 [3, 524288], P(None, 'tile'), may hold values from -4 to 4
Outputs:
- pose_step: float32 [6, 1024], P(None, 'tile')
Inputs may be any that keep to these rules, and one draw needn't show every extreme that they name: `intersection`: within the blocks of one device (each aligned run of 128 rows), no index is named more than 16 times, a bound that some block reaches.
All inputs are finite; a program needn't handle non-finite values.
Results may differ from a plain program's by a relative error of at most 0.0003.
Values sent between devices are 32-bit elements; how exact they have to be, the bound alone decides.
A program may use at most 64 MiB of HBM per device.

v0:
```python
import jax
import jax.numpy as jnp
from jax import lax
from jax.experimental import pallas as pl
from jax.experimental.pallas import tpu as pltpu
from jax.sharding import PartitionSpec as P

SCANS_DEV = 64
TARGET_PTS = 512
DAMPING = 0.1
LANES = 128
PAIR = 32
PRECISE = lax.Precision.HIGHEST
MESH = pl.DeviceIdType.MESH
VMEM = pl.BlockSpec(memory_space=pltpu.VMEM)
SMEM = pl.BlockSpec(memory_space=pltpu.SMEM)


def plan_kernel(dest, chosen, block, ids, seg):
    tiles = ids.shape[0]
    blocks = dest.shape[1]
    cap = seg.shape[0] * 8
    per_scan = blocks // SCANS_DEV
    f32 = jnp.float32
    hit = dest[...] == lax.broadcasted_iota(jnp.int32, (tiles, blocks), 0)
    first = lax.broadcasted_iota(jnp.int32, (blocks, blocks), 0)
    second = lax.broadcasted_iota(jnp.int32, (blocks, blocks), 1)
    rank = jnp.dot(
        hit.astype(f32), (first <= second).astype(f32), preferred_element_type=f32
    ).astype(jnp.int32)
    rank = jnp.where(hit, rank, 0)
    place = lax.broadcasted_iota(jnp.int32, (tiles, blocks), 1).astype(f32) + 1.0
    wanted = chosen[...].astype(f32) + 1.0
    lane = lax.broadcasted_iota(jnp.int32, (tiles, LANES), 1)
    at = jnp.zeros((tiles, LANES), f32)
    named = jnp.zeros((tiles, LANES), f32)
    for r in range(cap):
        mine = rank == r + 1
        at = jnp.where(
            lane == r, jnp.sum(jnp.where(mine, place, 0.0), axis=1, keepdims=True), at
        )
        named = jnp.where(
            lane == r, jnp.sum(jnp.where(mine, wanted, 0.0), axis=1, keepdims=True), named
        )
    at = at.astype(jnp.int32) - 1
    named = named.astype(jnp.int32) - 1
    block[...] = at
    scan = jnp.where(at >= 0, at // per_scan, -1)
    for t in range(tiles):
        ids[t] = named[t : t + 1]
    for g in range(cap // 8):
        seg[g : g + 1, :] = jnp.concatenate(
            [scan[t : t + 1, g * 8 : g * 8 + 8] for t in range(tiles)], axis=1
        )


def near_first(tiles, me, start, act):
    def one(j, c):
        k = (j + 1) // 2
        t = me + k * (2 * (j % 2) - 1)

        @pl.when((t >= 0) & (t < tiles))
        def _():
            act(t, j)

        return c

    lax.fori_loop(start, 2 * tiles - 1, one, 0)


def cross(u, v):
    return [
        u[1] * v[2] - u[2] * v[1],
        u[2] * v[0] - u[0] * v[2],
        u[0] * v[1] - u[1] * v[0],
    ]


def upper(vec):
    return [(a, b) for a in range(6) for b in range(a, 6)]


def main_kernel(
    block, sp, mt, ids, seg, tp, tn, out,
    pts, idx, got_pts, got_idx, got_ids, named, table, picked, own, far, back, tot, partner,
    ps, pr, qs, qr, js, jr, ss, rs, ls, gs, gr,
):
    tiles, _, cap, points = pts.shape
    me = lax.axis_index("tile")
    other = 1 - lax.axis_index("grp")
    barrier = pltpu.get_barrier_semaphore()

    def greet(k, c):
        to = lax.rem(me + k, tiles)
        pl.semaphore_signal(barrier, inc=1, device_id={"tile": to}, device_id_type=MESH)
        return c

    lax.fori_loop(1, tiles, greet, 0)
    pl.semaphore_signal(barrier, inc=1, device_id={"grp": other}, device_id_type=MESH)
    pl.semaphore_wait(barrier, tiles)

    def remote(src, dst, send, recv, to, frm):
        return pltpu.make_async_remote_copy(
            src.at[to], dst.at[frm], send.at[to], recv.at[frm], {"tile": to}, MESH
        )

    def id_copy(to, frm):
        return remote(ids, got_ids, js, jr, to, frm)

    def idx_copy(to, frm):
        return remote(idx, got_idx, qs, qr, to, frm)

    def pts_copy(to, frm):
        return remote(pts, got_pts, ps, pr, to, frm)

    def own_copy(to, frm):
        return remote(own, back, ss, rs, to, frm)

    near_first(tiles, me, 1, lambda t, j: id_copy(t, me).start())

    def pack(t, pts_to, idx_to):
        for r in range(cap):
            b = block[t, r]
            used = jnp.minimum(b, 0) + 1
            for h in range(points // LANES):
                span = slice(h * LANES, (h + 1) * LANES)
                at = jnp.maximum(b, 0) * (points // LANES) + h
                for a in range(3):
                    pts_to[t, a, r : r + 1, span] = sp[a, at]
                idx_to[t, r : r + 1, span] = mt[at] * used + (used - 1)

    def at_step(j):
        return me + (j + 1) // 2 * (2 * (j % 2) - 1)

    def pack_send(j, c):
        t = at_step(j)

        @pl.when((j < 2 * tiles - 1) & (t >= 0) & (t < tiles))
        def _():
            pack(t, pts, idx)

        u = at_step(j - 1)

        @pl.when((j > 1) & (u >= 0) & (u < tiles))
        def _():
            idx_copy(u, me).start()
            pts_copy(u, me).start()

        return c

    lax.fori_loop(1, 2 * tiles, pack_send, 0)
    self_ids = pltpu.make_async_copy(ids.at[me], got_ids.at[me], ls.at[0])
    self_ids.start()
    pack(me, got_pts, got_idx)

    def fill(s, c):
        cols = pl.ds(pl.multiple_of(s * TARGET_PTS, TARGET_PTS), TARGET_PTS)
        table[s, 0:3, :] = tp[:, cols]
        table[s, 3:6, :] = tn[:, cols]
        return c

    lax.fori_loop(0, SCANS_DEV, fill, 0, unroll=4)
    tot[...] = jnp.zeros(tot.shape, jnp.float32)
    self_ids.wait()
    near_first(tiles, me, 1, lambda t, j: id_copy(t, t).wait_recv())
    load_ids = pltpu.make_async_copy(got_ids, named, ls.at[1])
    load_ids.start()
    load_ids.wait()
    lane = lax.broadcasted_iota(jnp.int32, (8, LANES), 1)
    scan = lax.broadcasted_iota(jnp.int32, (SCANS_DEV, cap), 0)

    def group(d, g):
        r0 = g * 8
        near = got_idx[d, r0 : r0 + 8, :]
        for j in range(8):
            tab = table.at[jnp.maximum(named[d, 0, r0 + j], 0)]
            for h in range(points // LANES):
                at = jnp.broadcast_to(near[j : j + 1, h * LANES : (h + 1) * LANES], (8, LANES))
                low = at & (LANES - 1)
                high = (at >> 7) & (TARGET_PTS // LANES - 1)
                res = None
                for q in range(TARGET_PTS // LANES):
                    part = jnp.take_along_axis(
                        tab[:, q * LANES : (q + 1) * LANES],
                        low,
                        axis=1,
                        mode="promise_in_bounds",
                    )
                    res = part if res is None else jnp.where(high == q, part, res)
                picked[g, h, j * 8 : j * 8 + 8, :] = res
        halves = []
        for h in range(points // LANES):
            span = slice(h * LANES, (h + 1) * LANES)
            good = near[:, span] >= 0
            p = [
                jnp.where(good, got_pts[d, a, r0 : r0 + 8, span], 0.0) for a in range(3)
            ]
            q = [picked[g, h, pl.ds(a, 8, stride=8), :] for a in range(3)]
            n = [
                jnp.where(good, picked[g, h, pl.ds(3 + a, 8, stride=8), :], 0.0)
                for a in range(3)
            ]
            mis = n[0] * (p[0] - q[0]) + n[1] * (p[1] - q[1]) + n[2] * (p[2] - q[2])
            halves.append((cross(p, n) + n, cross(q, n) + n, mis))
        own_row = jnp.zeros((8, LANES), jnp.float32)
        far_row = jnp.zeros((8, LANES), jnp.float32)

        def total(make):
            acc = None
            for half in halves:
                acc = make(half) if acc is None else acc + make(half)
            return jnp.sum(acc, axis=1, keepdims=True)

        for f, (a, b) in enumerate(upper(6)):
            s = total(lambda v: v[0][a] * v[0][b])
            own_row = jnp.where(lane == PAIR * g + f, s, own_row)
            if a < 3:
                s = total(lambda v: v[1][a] * v[1][b])
            far_row = jnp.where(lane == f, s, far_row)
        for a in range(6):
            s = total(lambda v: v[0][a] * v[2])
            own_row = jnp.where(lane == PAIR * g + 21 + a, s, own_row)
            if a < 3:
                s = total(lambda v: v[1][a] * v[2])
            far_row = jnp.where(lane == 21 + a, -s, far_row)
        far[r0 : r0 + 8, :] = far_row
        return own_row

    def work(t, j):
        @pl.when(j > 0)
        def _():
            idx_copy(t, t).wait_recv()
            pts_copy(t, t).wait_recv()

        row = group(t, 0)
        for g in range(1, cap // 8):
            row = row + group(t, g)
        own[t] = row

        @pl.when(j == 0)
        def _():
            back[me] = own[me]

        @pl.when(j > 0)
        def _():
            own_copy(t, me).start()

        here = (scan == got_ids[t][:, :cap]).astype(jnp.float32)
        tot[...] += jnp.dot(
            here, far[...], precision=PRECISE, preferred_element_type=jnp.float32
        )

    near_first(tiles, me, 0, work)
    near_first(tiles, me, 1, lambda t, j: own_copy(t, t).wait_recv())
    wide = lax.broadcasted_iota(jnp.int32, (SCANS_DEV, tiles * 8), 0)
    rows = back[...].reshape(tiles * 8, LANES)
    sums = tot[...]
    for g in range(cap // 8):
        here = (wide == seg[g : g + 1, :]).astype(jnp.float32)
        part = jnp.dot(here, rows, precision=PRECISE, preferred_element_type=jnp.float32)
        if g > 0:
            part = pltpu.roll(part, LANES - PAIR * g, 1)
        sums = sums + part
    tot[...] = sums
    swap = pltpu.make_async_remote_copy(tot, partner, gs, gr, {"grp": other}, MESH)
    swap.start()

    def drain(t, j):
        for copy in (id_copy, idx_copy, pts_copy, own_copy):
            copy(t, me).wait_send()

    near_first(tiles, me, 1, drain)
    swap.wait()
    full = jnp.transpose(tot[...] + partner[...])
    for a, row in enumerate(solve_rows([full[f : f + 1, :] for f in range(27)])):
        out[a : a + 1, :] = row


def solve_rows(rows):
    entries = {}
    for f, (a, b) in enumerate(upper(6)):
        entries[a, b] = rows[f]
    traced = entries[0, 0]
    for a in range(1, 6):
        traced = traced + entries[a, a]
    shift_by = DAMPING * traced / 6.0
    for a in range(6):
        entries[a, a] = entries[a, a] + shift_by
    values = [-rows[21 + a] for a in range(6)]
    for k in range(6):
        for a in range(k + 1, 6):
            factor = entries[k, a] / entries[k, k]
            for b in range(a, 6):
                entries[a, b] = entries[a, b] - factor * entries[k, b]
            values[a] = values[a] - factor * values[k]
    result = [None] * 6
    for a in range(5, -1, -1):
        running = values[a]
        for b in range(a + 1, 6):
            running = running - entries[a, b] * result[b]
        result[a] = running / entries[a, a]
    return result


def body(source_points, intersection, target_scan, matches, target_points, target_normals):
    tiles = lax.axis_size("tile")
    blocks = intersection.shape[1]
    points = source_points.shape[2] // blocks
    cap = -(-(2 * blocks // tiles) // 8) * 8
    f32, i32 = jnp.float32, jnp.int32
    shape = jax.ShapeDtypeStruct
    many = pltpu.SemaphoreType.DMA((tiles,))
    pts_t, idx_t = (tiles, 3, cap, points), (tiles, cap, points)
    ids_t, sums_t = (tiles, 1, LANES), (SCANS_DEV, LANES)
    block, ids, seg = pl.pallas_call(
        plan_kernel,
        out_shape=(
            shape((tiles, LANES), i32),
            shape(ids_t, i32),
            shape((cap // 8, tiles * 8), i32),
        ),
        in_specs=[VMEM, VMEM],
        out_specs=(VMEM, VMEM, VMEM),
        name="plan",
    )(intersection.reshape(1, blocks), target_scan)
    return pl.pallas_call(
        main_kernel,
        out_shape=shape((6, SCANS_DEV), f32),
        in_specs=[SMEM] + [VMEM] * 6,
        out_specs=VMEM,
        scratch_shapes=[
            pltpu.VMEM(pts_t, f32),
            pltpu.VMEM(idx_t, i32),
            pltpu.VMEM(pts_t, f32),
            pltpu.VMEM(idx_t, i32),
            pltpu.VMEM(ids_t, i32),
            pltpu.SMEM(ids_t, i32),
            pltpu.VMEM((SCANS_DEV, 8, TARGET_PTS), f32),
            pltpu.VMEM((cap // 8, points // LANES, 64, LANES), f32),
            pltpu.VMEM((tiles, 8, LANES), f32),
            pltpu.VMEM((cap, LANES), f32),
            pltpu.VMEM((tiles, 8, LANES), f32),
            pltpu.VMEM(sums_t, f32),
            pltpu.VMEM(sums_t, f32),
        ]
        + [many] * 8
        + [pltpu.SemaphoreType.DMA((2,)), pltpu.SemaphoreType.DMA, pltpu.SemaphoreType.DMA],
        compiler_params=pltpu.CompilerParams(collective_id=0, has_side_effects=True),
        name="main",
    )(
        block,
        source_points.reshape(3, -1, 1, LANES),
        matches.reshape(-1, 1, LANES),
        ids,
        seg,
        target_points,
        target_normals,
    )


def solution(mesh):
    in_specs = (
        P("grp", None, "tile"),
        P("grp", "tile", None),
        P("grp", "tile"),
        P("grp", "tile"),
        P(None, "tile"),
        P(None, "tile"),
    )
    out_specs = P(None, "tile")
    return jax.shard_map(body, mesh=mesh, in_specs=in_specs, out_specs=out_specs, check_vma=False)
```

profile of v0, /device:TPU:0, one launch (start us, length us, event | category | flops | bytes accessed | tf_op | source)
XLA Modules:
  0.0 49.2 jit_solution(6162420462927794652)
XLA Ops:
  0.0 1.6 %plan.1 = (s32[16,128]{1,0:T(8,128)}, s32[16,1,128]{2,1,0:T(1,128)}, s32[2,128]{1,0:T(2,128)}) custom-call(s32[1,128]{1,0:T(1,128)} %bitcast.5, s32[1,128]{1,0:T(1,128)} %chosen.1), custom_call_target="tpu_custom_call" | custom-call | tf_op jit(solution)/shard_map/plan/pallas_call | solution.py:315
  1.6 46.3 %main.1 = f32[6,64]{1,0:T(8,128)} custom-call(s32[16,128]{1,0:T(8,128)} %get-tuple-element.8.block, f32[3,256,1,128]{3,2,1,0:T(1,128)} %bitcast.3, s32[256,1,128]{2,1,0:T(1,128)} %bitcast.4, s32[16,1,128]{2,1,0:T(1,128)} %get-tuple-element.9.ids, s32[2,128]{1,0:T(2,128)} %get-tuple-element.10.seg, f32[3,32768]{1,0:T(4,128)} %tp.1, f32[3,32768]{1,0:T(4,128)} %tn.1), custom_call_target="tpu_custom_call" | custom-call | tf_op jit(solution)/shard_map/main/pallas_call | solution.py:326
  48.0 1.3 %copy.8 = f32[6,64]{1,0:T(8,128)} copy(f32[6,64]{1,0:T(8,128)} %main.1) | data formatting | bytes 3072
where the time goes:
time: 49.4 us; the launch traced here: 49.2 us
  Pallas kernels  47.9 us (97%)
  local copies, waits for them, and re-layouts  1.27 us (3%)
    pallas_call x1, Pallas kernels, body(): pl.pallas_call(main_kernel, out_shape=shape((6, SCANS_DEV), f32), in_spec...  46.3 us
    pallas_call x1, Pallas kernels, body(): pl.pallas_call(plan_kernel, out_shape=(shape((tiles, LANES), i32), shape(...  1.61 us
    unnamed x1, local copies, waits for them, and re-layouts  1.27 us

commit v1 on v0

--- a/solution.py
+++ b/solution.py
@@ -10,13 +10,14 @@
 DAMPING = 0.1
 LANES = 128
 PAIR = 32
+AHEAD = 4
 PRECISE = lax.Precision.HIGHEST
 MESH = pl.DeviceIdType.MESH
 VMEM = pl.BlockSpec(memory_space=pltpu.VMEM)
-SMEM = pl.BlockSpec(memory_space=pltpu.SMEM)
-
-
-def plan_kernel(dest, chosen, block, ids, seg):
+ANY = pl.BlockSpec(memory_space=pl.ANY)
+
+
+def plan(dest, chosen, block, ids, seg):
     tiles = ids.shape[0]
     blocks = dest.shape[1]
     cap = seg.shape[0] * 8
@@ -54,18 +55,18 @@
         )
 
 
-def near_first(tiles, me, start, act):
-    def one(j, c):
-        k = (j + 1) // 2
-        t = me + k * (2 * (j % 2) - 1)
-
-        @pl.when((t >= 0) & (t < tiles))
-        def _():
-            act(t, j)
-
-        return c
-
-    lax.fori_loop(start, 2 * tiles - 1, one, 0)
+def flip(me, k, tiles):
+    other, bit = 0, 1
+    while bit < tiles:
+        other = other + (me // bit + k // bit) % 2 * bit
+        bit *= 2
+    return other
+
+
+def partner_at(j, me, tiles):
+    odd = j % 2
+    k = odd * (tiles - (j + 1) // 2) + (1 - odd) * (tiles // 2 - j // 2) * jnp.minimum(j, 1)
+    return flip(me, k, tiles)
 
 
 def cross(u, v):
@@ -81,11 +82,13 @@
 
 
 def main_kernel(
-    block, sp, mt, ids, seg, tp, tn, out,
+    dest_in, chosen_in, sp_in, mt_in, tp_in, tn_in, out,
+    dest, chosen, sp, mt, tp, tn, places, block, ids, seg,
     pts, idx, got_pts, got_idx, got_ids, named, table, picked, own, far, back, tot, partner,
     ps, pr, qs, qr, js, jr, ss, rs, ls, gs, gr,
 ):
     tiles, _, cap, points = pts.shape
+    blocks = dest.shape[1]
     me = lax.axis_index("tile")
     other = 1 - lax.axis_index("grp")
     barrier = pltpu.get_barrier_semaphore()
@@ -97,7 +100,14 @@
 
     lax.fori_loop(1, tiles, greet, 0)
     pl.semaphore_signal(barrier, inc=1, device_id={"grp": other}, device_id_type=MESH)
-    pl.semaphore_wait(barrier, tiles)
+    loads = [
+        pltpu.make_async_copy(src, dst, ls.at[i])
+        for i, (src, dst) in enumerate(
+            [(dest_in, dest), (chosen_in, chosen), (sp_in, sp), (mt_in, mt), (tp_in, tp), (tn_in, tn)]
+        )
+    ]
+    for load in loads:
+        load.start()
 
     def remote(src, dst, send, recv, to, frm):
         return pltpu.make_async_remote_copy(
@@ -116,7 +126,12 @@
     def own_copy(to, frm):
         return remote(own, back, ss, rs, to, frm)
 
-    near_first(tiles, me, 1, lambda t, j: id_copy(t, me).start())
+    def each(start, stop, act):
+        def one(j, c):
+            act(partner_at(j, me, tiles), j)
+            return c
+
+        lax.fori_loop(start, stop, one, 0)
 
     def pack(t, pts_to, idx_to):
         for r in range(cap):
@@ -124,34 +139,44 @@
             used = jnp.minimum(b, 0) + 1
             for h in range(points // LANES):
                 span = slice(h * LANES, (h + 1) * LANES)
-                at = jnp.maximum(b, 0) * (points // LANES) + h
+                at = jnp.clip(b, 0, blocks - 1) * (points // LANES) + h
                 for a in range(3):
                     pts_to[t, a, r : r + 1, span] = sp[a, at]
                 idx_to[t, r : r + 1, span] = mt[at] * used + (used - 1)
 
-    def at_step(j):
-        return me + (j + 1) // 2 * (2 * (j % 2) - 1)
-
-    def pack_send(j, c):
-        t = at_step(j)
-
-        @pl.when((j < 2 * tiles - 1) & (t >= 0) & (t < tiles))
+    def send(t):
+        idx_copy(t, me).start()
+        pts_copy(t, me).start()
+
+    loads[0].wait()
+    loads[1].wait()
+    plan(dest, chosen, places, ids, seg)
+    to_smem = pltpu.make_async_copy(places, block, ls.at[6])
+    to_smem.start()
+    loads[2].wait()
+    loads[3].wait()
+    to_smem.wait()
+    ahead = min(AHEAD, tiles - 1)
+    each(1, ahead + 1, lambda t, j: pack(t, pts, idx))
+    pl.semaphore_wait(barrier, tiles)
+    each(1, tiles, lambda t, j: id_copy(t, me).start())
+    each(1, ahead + 1, lambda t, j: send(t))
+
+    def pack_send(t, j):
+        @pl.when(j < tiles)
         def _():
             pack(t, pts, idx)
 
-        u = at_step(j - 1)
-
-        @pl.when((j > 1) & (u >= 0) & (u < tiles))
-        def _():
-            idx_copy(u, me).start()
-            pts_copy(u, me).start()
-
-        return c
-
-    lax.fori_loop(1, 2 * tiles, pack_send, 0)
-    self_ids = pltpu.make_async_copy(ids.at[me], got_ids.at[me], ls.at[0])
+        @pl.when(j > ahead + 1)
+        def _():
+            send(partner_at(j - 1, me, tiles))
+
+    each(ahead + 1, tiles + 1, pack_send)
+    self_ids = pltpu.make_async_copy(ids.at[me], got_ids.at[me], ls.at[7])
     self_ids.start()
     pack(me, got_pts, got_idx)
+    loads[4].wait()
+    loads[5].wait()
 
     def fill(s, c):
         cols = pl.ds(pl.multiple_of(s * TARGET_PTS, TARGET_PTS), TARGET_PTS)
@@ -162,8 +187,8 @@
     lax.fori_loop(0, SCANS_DEV, fill, 0, unroll=4)
     tot[...] = jnp.zeros(tot.shape, jnp.float32)
     self_ids.wait()
-    near_first(tiles, me, 1, lambda t, j: id_copy(t, t).wait_recv())
-    load_ids = pltpu.make_async_copy(got_ids, named, ls.at[1])
+    each(1, tiles, lambda t, j: id_copy(t, t).wait_recv())
+    load_ids = pltpu.make_async_copy(got_ids, named, ls.at[8])
     load_ids.start()
     load_ids.wait()
     lane = lax.broadcasted_iota(jnp.int32, (8, LANES), 1)
@@ -173,7 +198,7 @@
         r0 = g * 8
         near = got_idx[d, r0 : r0 + 8, :]
         for j in range(8):
-            tab = table.at[jnp.maximum(named[d, 0, r0 + j], 0)]
+            tab = table.at[jnp.clip(named[d, 0, r0 + j], 0, SCANS_DEV - 1)]
             for h in range(points // LANES):
                 at = jnp.broadcast_to(near[j : j + 1, h * LANES : (h + 1) * LANES], (8, LANES))
                 low = at & (LANES - 1)
@@ -250,8 +275,8 @@
             here, far[...], precision=PRECISE, preferred_element_type=jnp.float32
         )
 
-    near_first(tiles, me, 0, work)
-    near_first(tiles, me, 1, lambda t, j: own_copy(t, t).wait_recv())
+    each(0, tiles, work)
+    each(1, tiles, lambda t, j: own_copy(t, t).wait_recv())
     wide = lax.broadcasted_iota(jnp.int32, (SCANS_DEV, tiles * 8), 0)
     rows = back[...].reshape(tiles * 8, LANES)
     sums = tot[...]
@@ -269,7 +294,7 @@
         for copy in (id_copy, idx_copy, pts_copy, own_copy):
             copy(t, me).wait_send()
 
-    near_first(tiles, me, 1, drain)
+    each(1, tiles, drain)
     swap.wait()
     full = jnp.transpose(tot[...] + partner[...])
     for a, row in enumerate(solve_rows([full[f : f + 1, :] for f in range(27)])):
@@ -311,24 +336,24 @@
     shape = jax.ShapeDtypeStruct
     many = pltpu.SemaphoreType.DMA((tiles,))
     pts_t, idx_t = (tiles, 3, cap, points), (tiles, cap, points)
+    rows = (3, blocks * points // LANES, 1, LANES)
     ids_t, sums_t = (tiles, 1, LANES), (SCANS_DEV, LANES)
-    block, ids, seg = pl.pallas_call(
-        plan_kernel,
-        out_shape=(
-            shape((tiles, LANES), i32),
-            shape(ids_t, i32),
-            shape((cap // 8, tiles * 8), i32),
-        ),
-        in_specs=[VMEM, VMEM],
-        out_specs=(VMEM, VMEM, VMEM),
-        name="plan",
-    )(intersection.reshape(1, blocks), target_scan)
     return pl.pallas_call(
         main_kernel,
         out_shape=shape((6, SCANS_DEV), f32),
-        in_specs=[SMEM] + [VMEM] * 6,
+        in_specs=[ANY] * 6,
         out_specs=VMEM,
         scratch_shapes=[
+            pltpu.VMEM((1, blocks), i32),
+            pltpu.VMEM((1, blocks), i32),
+            pltpu.VMEM(rows, f32),
+            pltpu.VMEM(rows[1:], i32),
+            pltpu.VMEM(target_points.shape, f32),
+            pltpu.VMEM(target_normals.shape, f32),
+            pltpu.VMEM((tiles, LANES), i32),
+            pltpu.SMEM((tiles, LANES), i32),
+            pltpu.VMEM(ids_t, i32),
+            pltpu.VMEM((cap // 8, tiles * 8), i32),
             pltpu.VMEM(pts_t, f32),
             pltpu.VMEM(idx_t, i32),
             pltpu.VMEM(pts_t, f32),
@@ -344,15 +369,14 @@
             pltpu.VMEM(sums_t, f32),
         ]
         + [many] * 8
-        + [pltpu.SemaphoreType.DMA((2,)), pltpu.SemaphoreType.DMA, pltpu.SemaphoreType.DMA],
+        + [pltpu.SemaphoreType.DMA((9,)), pltpu.SemaphoreType.DMA, pltpu.SemaphoreType.DMA],
         compiler_params=pltpu.CompilerParams(collective_id=0, has_side_effects=True),
         name="main",
     )(
-        block,
-        source_points.reshape(3, -1, 1, LANES),
-        matches.reshape(-1, 1, LANES),
-        ids,
-        seg,
+        intersection.reshape(1, blocks),
+        target_scan,
+        source_points.reshape(rows),
+        matches.reshape(rows[1:]),
         target_points,
         target_normals,
     )

time: 49.4 us -> 40.6 us (0.82)
  Pallas kernels: 47.9 us -> 39.1 us
    pallas_call x1, Pallas kernels: 46.3 us -> 39.1 us  [body(): pl.pallas_call(main_kernel, out_shape=shape((6, SCANS_DEV), f32), in_spec...]
    pallas_call x1 -> x0, Pallas kernels: 1.61 us -> none  [body(): pl.pallas_call(plan_kernel, out_shape=(shape((tiles, LANES), i32), shape(...]
where the time goes in v1:
time: 40.6 us; the launch traced here: 40.4 us
  Pallas kernels  39.1 us (96%)
  local copies, waits for them, and re-layouts  1.28 us (3%)
    pallas_call x1, Pallas kernels, body(): pl.pallas_call(main_kernel, out_shape=shape((6, SCANS_DEV), f32), in_spec...  39.1 us
    unnamed x1, local copies, waits for them, and re-layouts  1.28 us

profile of v1, /device:TPU:0, one launch (start us, length us, event | category | flops | bytes accessed | tf_op | source)
XLA Modules:
  0.0 40.4 jit_solution(7567312091837700874)
XLA Ops:
  0.0 39.1 %main.1 = f32[6,64]{1,0:T(8,128)} custom-call(s32[1,128]{1,0:T(1,128)} %bitcast.5, s32[1,128]{1,0:T(1,128)} %chosen_in.1, f32[3,256,1,128]{3,2,1,0:T(1,128)} %bitcast.3, s32[256,1,128]{2,1,0:T(1,128)} %bitcast.4, f32[3,32768]{1,0:T(4,128)} %tp_in.1, f32[3,32768]{1,0:T(4,128)} %tn_in.1), custom_call_target="tpu_custom_call" | custom-call | tf_op jit(solution)/shard_map/main/pallas_call | solution.py:341
  39.1 1.3 %copy.8 = f32[6,64]{1,0:T(8,128)} copy(f32[6,64]{1,0:T(8,128)} %main.1) | data formatting | bytes 3072

commit v2 on v1

--- a/solution.py
+++ b/solution.py
@@ -63,10 +63,24 @@
     return other
 
 
-def partner_at(j, me, tiles):
-    odd = j % 2
-    k = odd * (tiles - (j + 1) // 2) + (1 - odd) * (tiles // 2 - j // 2) * jnp.minimum(j, 1)
-    return flip(me, k, tiles)
+def send_at(j, me, tiles):
+    half, quarter = tiles // 2, tiles // 4
+    i = j // 2
+    far = (3 - i % 2) * quarter + quarter - 1 - i // 2
+    return flip(me, jnp.where(j % 2 == 1, far, half - i), tiles)
+
+
+def recv_at(j, me, tiles):
+    half, quarter = tiles // 2, tiles // 4
+    place = me // quarter
+    inner = (place // 2 + place) % 2
+    last = j // (tiles - 1)
+    i = j // 2 - 1 + last
+    second = i // quarter
+    code = 3 - (inner + second) % 2
+    far = code * quarter + quarter - 1 - i % quarter
+    near = (half - (j + 1) // 2) * jnp.minimum(j, 1)
+    return flip(me, jnp.where((j > 0) & (j % 2 - last == 0), far, near), tiles)
 
 
 def cross(u, v):
@@ -126,9 +140,9 @@
     def own_copy(to, frm):
         return remote(own, back, ss, rs, to, frm)
 
-    def each(start, stop, act):
+    def each(start, stop, act, at=send_at):
         def one(j, c):
-            act(partner_at(j, me, tiles), j)
+            act(at(j, me, tiles), j)
             return c
 
         lax.fori_loop(start, stop, one, 0)
@@ -169,7 +183,7 @@
 
         @pl.when(j > ahead + 1)
         def _():
-            send(partner_at(j - 1, me, tiles))
+            send(send_at(j - 1, me, tiles))
 
     each(ahead + 1, tiles + 1, pack_send)
     self_ids = pltpu.make_async_copy(ids.at[me], got_ids.at[me], ls.at[7])
@@ -275,7 +289,7 @@
             here, far[...], precision=PRECISE, preferred_element_type=jnp.float32
         )
 
-    each(0, tiles, work)
+    each(0, tiles, work, recv_at)
     each(1, tiles, lambda t, j: own_copy(t, t).wait_recv())
     wide = lax.broadcasted_iota(jnp.int32, (SCANS_DEV, tiles * 8), 0)
     rows = back[...].reshape(tiles * 8, LANES)

time: 40.6 us -> 38.6 us (0.951)
  the two profiles are of different devices: /device:TPU:0 before, /device:TPU:9 now
where the time goes in v2:
time: 38.6 us; the launch traced here: 38.4 us
  Pallas kernels  37.1 us (96%)
  local copies, waits for them, and re-layouts  1.28 us (3%)
    pallas_call x1, Pallas kernels, body(): pl.pallas_call(main_kernel, out_shape=shape((6, SCANS_DEV), f32), in_spec...  37.1 us
    unnamed x1, local copies, waits for them, and re-layouts  1.28 us

profile of v2, /device:TPU:9, one launch (start us, length us, event | category | flops | bytes accessed | tf_op | source)
XLA Modules:
  0.0 38.4 jit_solution(13905277480230121143)
XLA Ops:
  0.0 37.1 %main.1 = f32[6,64]{1,0:T(8,128)} custom-call(s32[1,128]{1,0:T(1,128)} %bitcast.5, s32[1,128]{1,0:T(1,128)} %chosen_in.1, f32[3,256,1,128]{3,2,1,0:T(1,128)} %bitcast.3, s32[256,1,128]{2,1,0:T(1,128)} %bitcast.4, f32[3,32768]{1,0:T(4,128)} %tp_in.1, f32[3,32768]{1,0:T(4,128)} %tn_in.1), custom_call_target="tpu_custom_call" | custom-call | tf_op jit(solution)/shard_map/main/pallas_call | solution.py:355
  37.1 1.3 %copy.8 = f32[6,64]{1,0:T(8,128)} copy(f32[6,64]{1,0:T(8,128)} %main.1) | data formatting | bytes 3072

commit v3 on v2

v3 whole, which is shorter than its diff:
```python
import jax
import jax.numpy as jnp
from jax import lax
from jax.experimental import pallas as pl
from jax.experimental.pallas import tpu as pltpu
from jax.sharding import PartitionSpec as P

SCANS_DEV = 64
TARGET_PTS = 512
DAMPING = 0.1
LANES = 128
PAIR = 32
AHEAD = 3
MESH = pl.DeviceIdType.MESH
VMEM = pl.BlockSpec(memory_space=pltpu.VMEM)
ANY = pl.BlockSpec(memory_space=pl.ANY)


def spread(to, rows, wide):
    for g in range(to.shape[0]):
        to[g : g + 1, :] = jnp.concatenate(
            [rows[t : t + 1, g * wide : (g + 1) * wide] for t in range(rows.shape[0])], axis=1
        )


def plan(dest, chosen, block, ids, seg):
    tiles = ids.shape[0]
    blocks = dest.shape[1]
    cap = seg.shape[0] * 4
    per_scan = blocks // SCANS_DEV
    f32 = jnp.float32
    hit = dest[...] == lax.broadcasted_iota(jnp.int32, (tiles, blocks), 0)
    first = lax.broadcasted_iota(jnp.int32, (blocks, blocks), 0)
    second = lax.broadcasted_iota(jnp.int32, (blocks, blocks), 1)
    rank = jnp.dot(
        hit.astype(f32), (first <= second).astype(f32), preferred_element_type=f32
    ).astype(jnp.int32)
    rank = jnp.where(hit, rank, 0)
    place = lax.broadcasted_iota(jnp.int32, (tiles, blocks), 1).astype(f32) + 1.0
    wanted = chosen[...].astype(f32) + 1.0
    lane = lax.broadcasted_iota(jnp.int32, (tiles, LANES), 1)
    at = jnp.zeros((tiles, LANES), f32)
    named = jnp.zeros((tiles, LANES), f32)
    for r in range(cap):
        mine = rank == r + 1
        at = jnp.where(
            lane == r, jnp.sum(jnp.where(mine, place, 0.0), axis=1, keepdims=True), at
        )
        named = jnp.where(
            lane == r, jnp.sum(jnp.where(mine, wanted, 0.0), axis=1, keepdims=True), named
        )
    at = at.astype(jnp.int32) - 1
    named = named.astype(jnp.int32) - 1
    spread(block, at, 8)
    scan = jnp.where(at >= 0, at // per_scan, -1)
    for t in range(tiles):
        ids[t] = named[t : t + 1]
    spread(seg, scan, 4)


def flip(me, k, tiles):
    other, bit = 0, 1
    while bit < tiles:
        other = other + (me // bit + k // bit) % 2 * bit
        bit *= 2
    return other


def send_at(j, me, tiles):
    half, quarter = tiles // 2, tiles // 4
    i = j // 2
    place = me // quarter
    inner = (place // 2 + place) % 2
    code = 3 - (inner * (1 - i // quarter) + (1 - inner) * (i % 2))
    low = inner * (i % quarter) + (1 - inner) * (i // 2)
    far = code * quarter + quarter - 1 - low
    return flip(me, jnp.where(j % 2 == 1, far, half - i), tiles)


def recv_at(j, me, tiles):
    half, quarter = tiles // 2, tiles // 4
    place = me // quarter
    inner = (place // 2 + place) % 2
    last = j // (tiles - 1)
    i = j // 2 - 1 + last
    second = i // quarter
    code = 3 - (inner + second) % 2
    far = code * quarter + quarter - 1 - i % quarter
    near = (half - (j + 1) // 2) * jnp.minimum(j, 1)
    return flip(me, jnp.where((j > 0) & (j % 2 - last == 0), far, near), tiles)


def pick(here, rows):
    bf16, f32 = jnp.bfloat16, jnp.float32
    parts = []
    for _ in range(3):
        parts.append(rows.astype(bf16))
        rows = rows - parts[-1].astype(f32)
    here = here.astype(f32).astype(bf16)
    return jnp.dot(
        jnp.concatenate([here] * 3, axis=1),
        jnp.concatenate(parts, axis=0),
        preferred_element_type=f32,
    )


def cross(u, v):
    return [
        u[1] * v[2] - u[2] * v[1],
        u[2] * v[0] - u[0] * v[2],
        u[0] * v[1] - u[1] * v[0],
    ]


def upper(vec):
    return [(a, b) for a in range(6) for b in range(a, 6)]


def main_kernel(
    dest_in, chosen_in, sp_in, mt_in, tp_in, tn_in, out,
    dest, chosen, sp, mt, tp, tn, places, block, ids, seg,
    seg_other, pts, got, got_ids, named, table, picked, own, far, back, tot, partner,
    pr, ps, js, jr, ss, rs, ls, hs, hr, gs, gr,
):
    tiles, _, cap, points = pts.shape
    blocks = dest.shape[1]
    me = lax.axis_index("tile")
    grp = lax.axis_index("grp")
    other = 1 - grp
    barrier = pltpu.get_barrier_semaphore()

    def greet(k, c):
        to = lax.rem(me + k, tiles)
        for side in range(2):
            pl.semaphore_signal(
                barrier, inc=1, device_id={"grp": side, "tile": to}, device_id_type=MESH
            )
        return c

    pl.semaphore_signal(barrier, inc=1, device_id={"grp": other}, device_id_type=MESH)
    lax.fori_loop(1, tiles, greet, 0)
    loads = [
        pltpu.make_async_copy(src, dst, ls.at[i])
        for i, (src, dst) in enumerate(
            [(dest_in, dest), (chosen_in, chosen), (sp_in, sp), (mt_in, mt), (tp_in, tp), (tn_in, tn)]
        )
    ]
    for load in loads:
        load.start()

    def remote(src, dst, send, recv, to, side=grp):
        return pltpu.make_async_remote_copy(
            src, dst, send, recv, {"grp": side, "tile": to}, MESH
        )

    def id_copy(t):
        return remote(ids.at[t], got_ids.at[me], js, jr, t)

    def pts_copy(to, frm):
        return remote(pts.at[to], got.at[frm], ps, pr.at[frm], to)

    def own_copy(t, side):
        return remote(own.at[t], back.at[grp * tiles + me], ss, rs, t, side)

    def all_of(src, dst, send, recv, count):
        span = pl.ds(0, count)
        return remote(src.at[span], dst.at[span], send, recv, me, other)

    seg_copy = remote(seg, seg_other, hs, hr, me, other)
    swap = remote(tot, partner, gs, gr, me, other)

    def each(start, stop, act, at=send_at):
        def one(j, c):
            act(at(j, me, tiles), j)
            return c

        lax.fori_loop(start, stop, one, 0)

    def pack(t, to, at_to):
        for r in range(cap):
            b = block[r // 8, t * 8 + r % 8]
            used = jnp.minimum(b, 0) + 1
            for h in range(points // LANES):
                span = slice(h * LANES, (h + 1) * LANES)
                at = jnp.clip(b, 0, blocks - 1) * (points // LANES) + h
                for a in range(3):
                    to[at_to, a, r : r + 1, span] = sp[a, at]
                to[at_to, 3, r : r + 1, span] = (mt[at] * used + (used - 1)).astype(jnp.float32)

    loads[0].wait()
    loads[1].wait()
    plan(dest, chosen, places, ids, seg)
    to_smem = pltpu.make_async_copy(places, block, ls.at[6])
    to_smem.start()
    loads[2].wait()
    loads[3].wait()
    to_smem.wait()
    ahead = min(AHEAD, tiles - 1)
    each(1, ahead + 1, lambda t, j: pack(t, pts, t))
    pl.semaphore_wait(barrier, 2 * tiles - 1)
    each(1, tiles, lambda t, j: id_copy(t).start())
    each(1, ahead + 1, lambda t, j: pts_copy(t, me).start())
    seg_copy.start()

    def pack_send(t, j):
        @pl.when(j < tiles)
        def _():
            pack(t, pts, t)

        @pl.when(j > ahead + 1)
        def _():
            pts_copy(send_at(j - 1, me, tiles), me).start()

    each(ahead + 1, tiles + 1, pack_send)
    self_ids = pltpu.make_async_copy(ids.at[me], got_ids.at[me], ls.at[7])
    self_ids.start()
    pack(me, got, me)
    loads[4].wait()
    loads[5].wait()

    chunks = TARGET_PTS // LANES - 1

    def fill(s, c):
        def cols(q):
            return pl.ds(pl.multiple_of(s * TARGET_PTS + q * LANES, LANES), LANES)

        for q in range(chunks):
            span = slice(q * LANES, (q + 1) * LANES)
            table[s, 0:3, span] = tp[:, cols(q)]
            table[s, 3:6, span] = tn[:, cols(q)]
            for r in range(2):
                ref, a = ((tp, 2 * q + r), (tn, 2 * q + r - 3))[2 * q + r > 2]
                table[s, 6 + r : 7 + r, span] = ref[a : a + 1, cols(chunks)]
        return c

    lax.fori_loop(0, SCANS_DEV, fill, 0, unroll=4)
    tot[...] = jnp.zeros(tot.shape, jnp.float32)
    self_ids.wait()
    all_of(ids, got_ids, js, jr, tiles - 1).wait_recv()
    load_ids = pltpu.make_async_copy(got_ids, named, ls.at[8])
    load_ids.start()
    load_ids.wait()
    lane = lax.broadcasted_iota(jnp.int32, (8, LANES), 1)
    scan = lax.broadcasted_iota(jnp.int32, (SCANS_DEV, cap), 0)
    halves_of = points // LANES

    def gather(d, g):
        r0 = g * 8
        near = got[d, 3, r0 : r0 + 8, :].astype(jnp.int32)
        for j in range(8):
            tab = table.at[jnp.clip(named[d, 0, r0 + j], 0, SCANS_DEV - 1)]
            for h in range(halves_of):
                at = jnp.broadcast_to(near[j : j + 1, h * LANES : (h + 1) * LANES], (8, LANES))
                low = at & (LANES - 1)
                for q in range(chunks):
                    picked[g, h, q, j * 8 : j * 8 + 8, :] = jnp.take_along_axis(
                        tab[:, q * LANES : (q + 1) * LANES],
                        low,
                        axis=1,
                        mode="promise_in_bounds",
                    )

    def group(d, g, far_to):
        r0 = g * 8
        near = got[d, 3, r0 : r0 + 8, :].astype(jnp.int32)
        halves = []
        for h in range(halves_of):
            span = slice(h * LANES, (h + 1) * LANES)
            good = near[:, span] >= 0
            chunk = (near[:, span] >> 7) & chunks
            rows = []
            for a in range(6):
                row = picked[g, h, a // 2, pl.ds(6 + a % 2, 8, stride=8), :]
                for q in range(chunks):
                    row = jnp.where(chunk == q, picked[g, h, q, pl.ds(a, 8, stride=8), :], row)
                rows.append(row)
            p = [
                jnp.where(good, got[d, a, r0 : r0 + 8, span], 0.0) for a in range(3)
            ]
            q = rows[:3]
            n = [jnp.where(good, row, 0.0) for row in rows[3:]]
            mis = n[0] * (p[0] - q[0]) + n[1] * (p[1] - q[1]) + n[2] * (p[2] - q[2])
            halves.append((cross(p, n) + n, cross(q, n) + n, mis))
        own_row = jnp.zeros((8, LANES), jnp.float32)
        far_row = jnp.zeros((8, LANES), jnp.float32)

        def total(make):
            acc = None
            for half in halves:
                acc = make(half) if acc is None else acc + make(half)
            return jnp.sum(acc, axis=1, keepdims=True)

        for f, (a, b) in enumerate(upper(6)):
            s = total(lambda v: v[0][a] * v[0][b])
            own_row = jnp.where(lane == PAIR * g + f, s, own_row)
            if a < 3:
                s = total(lambda v: v[1][a] * v[1][b])
            far_row = jnp.where(lane == f, s, far_row)
        for a in range(6):
            s = total(lambda v: v[0][a] * v[2])
            own_row = jnp.where(lane == PAIR * g + 21 + a, s, own_row)
            if a < 3:
                s = total(lambda v: v[1][a] * v[2])
            far_row = jnp.where(lane == 21 + a, -s, far_row)
        far[far_to, r0 : r0 + 8, :] = far_row
        return own_row

    def scatter(t, far_at):
        tot[...] += pick(scan == got_ids[t][:, :cap], far[far_at])

    far[1] = jnp.zeros(far.shape[1:], jnp.float32)

    def work(t, j):
        @pl.when(j > 0)
        def _():
            pts_copy(t, t).wait_recv()

        scatter(recv_at(jnp.maximum(j - 1, 0), me, tiles), (j + 1) % 2)
        for g in range(cap // 8):
            gather(t, g)

        @pl.when(j >= 0)
        def _():
            row = group(t, 0, j % 2)
            for g in range(1, cap // 8):
                row = row + group(t, g, j % 2)
            own[t] = row[:4] + pltpu.roll(row, LANES // 2, 1)[4:]

        @pl.when(j == 0)
        def _():
            back[grp * tiles + me] = own[t]

        @pl.when(j > 0)
        def _():
            own_copy(t, grp).start()

        own_copy(t, other).start()

    each(0, tiles, work, recv_at)
    scatter(recv_at(tiles - 1, me, tiles), (tiles - 1) % 2)
    seg_copy.wait_recv()
    all_of(pts, got, ps, pr.at[me], tiles - 1).wait_send()
    all_of(ids, got_ids, js, jr, tiles - 1).wait_send()
    seg_copy.wait_send()
    swap.start()
    all_of(back, back, ss, rs, 2 * tiles - 1).wait_recv()
    sums = tot[...]
    wide = lax.broadcasted_iota(jnp.int32, (SCANS_DEV, tiles * 4), 0)
    for mine, at in ((seg, grp), (seg_other, other)):
        rows = back[pl.ds(at * tiles, tiles)].reshape(tiles * 4, LANES)
        for g in range(cap // 8):
            for h in range(2):
                part = pick(wide == mine[2 * g + h : 2 * g + h + 1, :], rows)
                if g + h > 0:
                    part = pltpu.roll(part, LANES - PAIR * g - LANES // 2 * h, 1)
                sums = sums + part
    all_of(back, back, ss, rs, 2 * tiles - 1).wait_send()
    swap.wait()
    full = jnp.transpose(sums + partner[...])
    for a, row in enumerate(solve_rows([full[f : f + 1, :] for f in range(27)])):
        out[a : a + 1, :] = row


def solve_rows(rows):
    entries = {}
    for f, (a, b) in enumerate(upper(6)):
        entries[a, b] = rows[f]
    traced = entries[0, 0]
    for a in range(1, 6):
        traced = traced + entries[a, a]
    shift_by = DAMPING * traced / 6.0
    for a in range(6):
        entries[a, a] = entries[a, a] + shift_by
    values = [-rows[21 + a] for a in range(6)]
    for k in range(6):
        for a in range(k + 1, 6):
            factor = entries[k, a] / entries[k, k]
            for b in range(a, 6):
                entries[a, b] = entries[a, b] - factor * entries[k, b]
            values[a] = values[a] - factor * values[k]
    result = [None] * 6
    for a in range(5, -1, -1):
        running = values[a]
        for b in range(a + 1, 6):
            running = running - entries[a, b] * result[b]
        result[a] = running / entries[a, a]
    return result


def body(source_points, intersection, target_scan, matches, target_points, target_normals):
    tiles = lax.axis_size("tile")
    blocks = intersection.shape[1]
    points = source_points.shape[2] // blocks
    cap = -(-(2 * blocks // tiles) // 8) * 8
    f32, i32 = jnp.float32, jnp.int32
    shape = jax.ShapeDtypeStruct
    pts_t = (tiles, 4, cap, points)
    rows = (3, blocks * points // LANES, 1, LANES)
    ids_t, sums_t = (tiles, 1, LANES), (SCANS_DEV, LANES)
    return pl.pallas_call(
        main_kernel,
        out_shape=shape((6, SCANS_DEV), f32),
        in_specs=[ANY] * 6,
        out_specs=VMEM,
        scratch_shapes=[
            pltpu.VMEM((1, blocks), i32),
            pltpu.VMEM((1, blocks), i32),
            pltpu.VMEM(rows, f32),
            pltpu.VMEM(rows[1:], i32),
            pltpu.VMEM(target_points.shape, f32),
            pltpu.VMEM(target_normals.shape, f32),
            pltpu.VMEM((cap // 8, tiles * 8), i32),
            pltpu.SMEM((cap // 8, tiles * 8), i32),
            pltpu.VMEM(ids_t, i32),
            pltpu.VMEM((cap // 4, tiles * 4), i32),
            pltpu.VMEM((cap // 4, tiles * 4), i32),
            pltpu.VMEM(pts_t, f32),
            pltpu.VMEM(pts_t, f32),
            pltpu.VMEM(ids_t, i32),
            pltpu.SMEM(ids_t, i32),
            pltpu.VMEM((SCANS_DEV, 8, TARGET_PTS - LANES), f32),
            pltpu.VMEM((cap // 8, points // LANES, TARGET_PTS // LANES - 1, 64, LANES), f32),
            pltpu.VMEM((tiles, 4, LANES), f32),
            pltpu.VMEM((2, cap, LANES), f32),
            pltpu.VMEM((2 * tiles, 4, LANES), f32),
            pltpu.VMEM(sums_t, f32),
            pltpu.VMEM(sums_t, f32),
        ]
        + [pltpu.SemaphoreType.DMA((tiles,))]
        + [pltpu.SemaphoreType.DMA] * 5
        + [pltpu.SemaphoreType.DMA((9,))]
        + [pltpu.SemaphoreType.DMA] * 4,
        compiler_params=pltpu.CompilerParams(collective_id=0, has_side_effects=True),
        name="main",
    )(
        intersection.reshape(1, blocks),
        target_scan,
        source_points.reshape(rows),
        matches.reshape(rows[1:]),
        target_points,
        target_normals,
    )


def solution(mesh):
    in_specs = (
        P("grp", None, "tile"),
        P("grp", "tile", None),
        P("grp", "tile"),
        P("grp", "tile"),
        P(None, "tile"),
        P(None, "tile"),
    )
    out_specs = P(None, "tile")
    return jax.shard_map(body, mesh=mesh, in_specs=in_specs, out_specs=out_specs, check_vma=False)
```

time: 38.6 us -> 36.7 us (0.951)
  the two profiles are of different devices: /device:TPU:9 before, /device:TPU:0 now
where the time goes in v3:
time: 36.7 us; the launch traced here: 36.3 us
  Pallas kernels  35 us (95%)
  local copies, waits for them, and re-layouts  1.28 us (3%)
    pallas_call x1, Pallas kernels, body(): pl.pallas_call(main_kernel, out_shape=shape((6, SCANS_DEV), f32), in_spec...  35 us
    unnamed x1, local copies, waits for them, and re-layouts  1.28 us

profile of v3, /device:TPU:0, one launch (start us, length us, event | category | flops | bytes accessed | tf_op | source)
XLA Modules:
  0.0 36.3 jit_solution(8936742215435545990)
XLA Ops:
  0.0 35.0 %main.1 = f32[6,64]{1,0:T(8,128)} custom-call(s32[1,128]{1,0:T(1,128)} %bitcast.5, s32[1,128]{1,0:T(1,128)} %chosen_in.1, f32[3,256,1,128]{3,2,1,0:T(1,128)} %bitcast.3, s32[256,1,128]{2,1,0:T(1,128)} %bitcast.4, f32[3,32768]{1,0:T(4,128)} %tp_in.1, f32[3,32768]{1,0:T(4,128)} %tn_in.1), custom_call_target="tpu_custom_call" | custom-call | tf_op jit(solution)/shard_map/main/pallas_call | solution.py:400
  35.0 1.3 %copy.8 = f32[6,64]{1,0:T(8,128)} copy(f32[6,64]{1,0:T(8,128)} %main.1) | data formatting | bytes 3072

commit v4 on v3

--- a/solution.py
+++ b/solution.py
@@ -399,7 +399,7 @@
     ids_t, sums_t = (tiles, 1, LANES), (SCANS_DEV, LANES)
     return pl.pallas_call(
         main_kernel,
-        out_shape=shape((6, SCANS_DEV), f32),
+        out_shape=pltpu.VMEM((6, SCANS_DEV), f32),
         in_specs=[ANY] * 6,
         out_specs=VMEM,
         scratch_shapes=[

time: 36.7 us -> 35.3 us (0.962)
  local copies, waits for them, and re-layouts: 1.28 us -> 0.6 us
  Pallas kernels: 35 us -> 34.5 us
    unnamed x1, local copies, waits for them, and re-layouts: 1.28 us -> 0.6 us
    pallas_call x1, Pallas kernels: 35 us -> 34.5 us  [body(): pl.pallas_call(main_kernel, out_shape=pltpu.VMEM((6, SCANS_DEV), f32), in...]
where the time goes in v4:
time: 35.3 us; the launch traced here: 35.1 us
  Pallas kernels  34.5 us (98%)
  local copies, waits for them, and re-layouts  0.6 us (2%)
    pallas_call x1, Pallas kernels, body(): pl.pallas_call(main_kernel, out_shape=pltpu.VMEM((6, SCANS_DEV), f32), in...  34.5 us

profile of v4, /device:TPU:0, one launch (start us, length us, event | category | flops | bytes accessed | tf_op | source)
XLA Modules:
  0.0 35.1 jit_solution(2674180084774538958)
XLA Ops:
  0.0 34.5 %main.1 = f32[6,64]{1,0:T(8,128)S(1)} custom-call(s32[1,128]{1,0:T(1,128)} %bitcast.5, s32[1,128]{1,0:T(1,128)} %chosen_in.1, f32[3,256,1,128]{3,2,1,0:T(1,128)} %bitcast.3, s32[256,1,128]{2,1,0:T(1,128)} %bitcast.4, f32[3,32768]{1,0:T(4,128)} %tp_in.1, f32[3,32768]{1,0:T(4,128)} %tn_in.1), custom_call_target="tpu_custom_call" | custom-call | tf_op jit(solution)/shard_map/main/pallas_call | solution.py:400
  34.5 0.6 %copy.8 = f32[6,64]{1,0:T(8,128)} copy(f32[6,64]{1,0:T(8,128)S(1)} %main.1) | data formatting | bytes 3072

commit v5 on v4

--- a/solution.py
+++ b/solution.py
@@ -10,7 +10,7 @@
 DAMPING = 0.1
 LANES = 128
 PAIR = 32
-AHEAD = 3
+AHEAD = 2
 MESH = pl.DeviceIdType.MESH
 VMEM = pl.BlockSpec(memory_space=pltpu.VMEM)
 ANY = pl.BlockSpec(memory_space=pl.ANY)
@@ -23,7 +23,7 @@
         )
 
 
-def plan(dest, chosen, block, ids, seg):
+def plan(dest, chosen, block, ids, seg, ready):
     tiles = ids.shape[0]
     blocks = dest.shape[1]
     cap = seg.shape[0] * 4
@@ -36,22 +36,20 @@
         hit.astype(f32), (first <= second).astype(f32), preferred_element_type=f32
     ).astype(jnp.int32)
     rank = jnp.where(hit, rank, 0)
+    lane = lax.broadcasted_iota(jnp.int32, (tiles, LANES), 1)
+
+    def listed(values):
+        out = jnp.zeros((tiles, LANES), f32)
+        for r in range(cap):
+            value = jnp.sum(jnp.where(rank == r + 1, values, 0.0), axis=1, keepdims=True)
+            out = jnp.where(lane == r, value, out)
+        return out.astype(jnp.int32) - 1
+
     place = lax.broadcasted_iota(jnp.int32, (tiles, blocks), 1).astype(f32) + 1.0
-    wanted = chosen[...].astype(f32) + 1.0
-    lane = lax.broadcasted_iota(jnp.int32, (tiles, LANES), 1)
-    at = jnp.zeros((tiles, LANES), f32)
-    named = jnp.zeros((tiles, LANES), f32)
-    for r in range(cap):
-        mine = rank == r + 1
-        at = jnp.where(
-            lane == r, jnp.sum(jnp.where(mine, place, 0.0), axis=1, keepdims=True), at
-        )
-        named = jnp.where(
-            lane == r, jnp.sum(jnp.where(mine, wanted, 0.0), axis=1, keepdims=True), named
-        )
-    at = at.astype(jnp.int32) - 1
-    named = named.astype(jnp.int32) - 1
+    at = listed(place)
     spread(block, at, 8)
+    ready()
+    named = listed(chosen[...].astype(f32) + 1.0)
     scan = jnp.where(at >= 0, at // per_scan, -1)
     for t in range(tiles):
         ids[t] = named[t : t + 1]
@@ -68,13 +66,14 @@
 
 def send_at(j, me, tiles):
     half, quarter = tiles // 2, tiles // 4
-    i = j // 2
+    i = jnp.where(j <= quarter, j - 1, jnp.where(j <= half + quarter, quarter + (j - quarter - 1) // 2, 0))
+    n = jnp.where(j <= half + quarter, (j - quarter) // 2, j - half)
     place = me // quarter
     inner = (place // 2 + place) % 2
     code = 3 - (inner * (1 - i // quarter) + (1 - inner) * (i % 2))
     low = inner * (i % quarter) + (1 - inner) * (i // 2)
     far = code * quarter + quarter - 1 - low
-    return flip(me, jnp.where(j % 2 == 1, far, half - i), tiles)
+    return flip(me, jnp.where((j <= quarter) | ((j <= half + quarter) & ((j - quarter) % 2 == 1)), far, half - n), tiles)
 
 
 def recv_at(j, me, tiles):
@@ -189,9 +188,8 @@
 
     loads[0].wait()
     loads[1].wait()
-    plan(dest, chosen, places, ids, seg)
     to_smem = pltpu.make_async_copy(places, block, ls.at[6])
-    to_smem.start()
+    plan(dest, chosen, places, ids, seg, to_smem.start)
     loads[2].wait()
     loads[3].wait()
     to_smem.wait()

time: 35.3 us -> 34.9 us (0.989)
  Pallas kernels: 34.5 us -> 34 us
    pallas_call x1, Pallas kernels: 34.5 us -> 34 us  [body(): pl.pallas_call(main_kernel, out_shape=pltpu.VMEM((6, SCANS_DEV), f32), in...]
where the time goes in v5:
time: 34.9 us; the launch traced here: 34.6 us
  Pallas kernels  34 us (97%)
  local copies, waits for them, and re-layouts  0.6 us (2%)
    pallas_call x1, Pallas kernels, body(): pl.pallas_call(main_kernel, out_shape=pltpu.VMEM((6, SCANS_DEV), f32), in...  34 us

profile of v5, /device:TPU:0, one launch (start us, length us, event | category | flops | bytes accessed | tf_op | source)
XLA Modules:
  0.0 34.6 jit_solution(2579569813336102529)
XLA Ops:
  0.0 34.0 %main.1 = f32[6,64]{1,0:T(8,128)S(1)} custom-call(s32[1,128]{1,0:T(1,128)} %bitcast.5, s32[1,128]{1,0:T(1,128)} %chosen_in.1, f32[3,256,1,128]{3,2,1,0:T(1,128)} %bitcast.3, s32[256,1,128]{2,1,0:T(1,128)} %bitcast.4, f32[3,32768]{1,0:T(4,128)} %tp_in.1, f32[3,32768]{1,0:T(4,128)} %tn_in.1), custom_call_target="tpu_custom_call" | custom-call | tf_op jit(solution)/shard_map/main/pallas_call | solution.py:398
  34.0 0.6 %copy.8 = f32[6,64]{1,0:T(8,128)} copy(f32[6,64]{1,0:T(8,128)S(1)} %main.1) | data formatting | bytes 3072

commit v6 on v5

--- a/solution.py
+++ b/solution.py
@@ -91,11 +91,15 @@
 
 def pick(here, rows):
     bf16, f32 = jnp.bfloat16, jnp.float32
+    return pick_by(here.astype(f32).astype(bf16), rows)
+
+
+def pick_by(here, rows):
+    bf16, f32 = jnp.bfloat16, jnp.float32
     parts = []
     for _ in range(3):
         parts.append(rows.astype(bf16))
         rows = rows - parts[-1].astype(f32)
-    here = here.astype(f32).astype(bf16)
     return jnp.dot(
         jnp.concatenate([here] * 3, axis=1),
         jnp.concatenate(parts, axis=0),
@@ -118,7 +122,7 @@
 def main_kernel(
     dest_in, chosen_in, sp_in, mt_in, tp_in, tn_in, out,
     dest, chosen, sp, mt, tp, tn, places, block, ids, seg,
-    seg_other, pts, got, got_ids, named, table, picked, own, far, back, tot, partner,
+    seg_other, pts, got, got_ids, named, table, picked, own, far, back, tot, partner, masks,
     pr, ps, js, jr, ss, rs, ls, hs, hr, gs, gr,
 ):
     tiles, _, cap, points = pts.shape
@@ -128,6 +132,15 @@
     other = 1 - grp
     barrier = pltpu.get_barrier_semaphore()
 
+    loads = [
+        pltpu.make_async_copy(src, dst, ls.at[i])
+        for i, (src, dst) in enumerate(
+            [(dest_in, dest), (chosen_in, chosen), (sp_in, sp), (mt_in, mt), (tp_in, tp), (tn_in, tn)]
+        )
+    ]
+    for load in loads[:4]:
+        load.start()
+
     def greet(k, c):
         to = lax.rem(me + k, tiles)
         for side in range(2):
@@ -138,13 +151,7 @@
 
     pl.semaphore_signal(barrier, inc=1, device_id={"grp": other}, device_id_type=MESH)
     lax.fori_loop(1, tiles, greet, 0)
-    loads = [
-        pltpu.make_async_copy(src, dst, ls.at[i])
-        for i, (src, dst) in enumerate(
-            [(dest_in, dest), (chosen_in, chosen), (sp_in, sp), (mt_in, mt), (tp_in, tp), (tn_in, tn)]
-        )
-    ]
-    for load in loads:
+    for load in loads[4:]:
         load.start()
 
     def remote(src, dst, send, recv, to, side=grp):
@@ -341,17 +348,21 @@
     all_of(ids, got_ids, js, jr, tiles - 1).wait_send()
     seg_copy.wait_send()
     swap.start()
+    wide = lax.broadcasted_iota(jnp.int32, (SCANS_DEV, tiles * 4), 0)
+    groups = cap // 4
+    for c, mine in enumerate((seg, seg_other)):
+        for g in range(groups):
+            here = wide == mine[g : g + 1, :]
+            masks[c * groups + g] = here.astype(jnp.float32).astype(jnp.bfloat16)
     all_of(back, back, ss, rs, 2 * tiles - 1).wait_recv()
     sums = tot[...]
-    wide = lax.broadcasted_iota(jnp.int32, (SCANS_DEV, tiles * 4), 0)
-    for mine, at in ((seg, grp), (seg_other, other)):
-        rows = back[pl.ds(at * tiles, tiles)].reshape(tiles * 4, LANES)
-        for g in range(cap // 8):
-            for h in range(2):
-                part = pick(wide == mine[2 * g + h : 2 * g + h + 1, :], rows)
-                if g + h > 0:
-                    part = pltpu.roll(part, LANES - PAIR * g - LANES // 2 * h, 1)
-                sums = sums + part
+    for g in range(groups):
+        for c, at in enumerate((grp, other)):
+            rows = back[pl.ds(at * tiles, tiles)].reshape(tiles * 4, LANES)
+            part = pick_by(masks[c * groups + g], rows)
+            if g > 0:
+                part = pltpu.roll(part, LANES - PAIR * (g // 2) - LANES // 2 * (g % 2), 1)
+            sums = sums + part
     all_of(back, back, ss, rs, 2 * tiles - 1).wait_send()
     swap.wait()
     full = jnp.transpose(sums + partner[...])
@@ -423,6 +434,7 @@
             pltpu.VMEM((2 * tiles, 4, LANES), f32),
             pltpu.VMEM(sums_t, f32),
             pltpu.VMEM(sums_t, f32),
+            pltpu.VMEM((cap // 2, SCANS_DEV, tiles * 4), jnp.bfloat16),
         ]
         + [pltpu.SemaphoreType.DMA((tiles,))]
         + [pltpu.SemaphoreType.DMA] * 5

time: 34.9 us -> 34.9 us (level)
  no operation moved by 1% of the time
where the time goes in v6:
time: 34.9 us; the launch traced here: 34.3 us
  Pallas kernels  33.7 us (97%)
  local copies, waits for them, and re-layouts  0.6 us (2%)
    pallas_call x1, Pallas kernels, body(): pl.pallas_call(main_kernel, out_shape=pltpu.VMEM((6, SCANS_DEV), f32), in...  33.7 us

profile of v6, /device:TPU:0, one launch (start us, length us, event | category | flops | bytes accessed | tf_op | source)
XLA Modules:
  0.0 34.3 jit_solution(15924804110444969660)
XLA Ops:
  0.0 33.7 %main.1 = f32[6,64]{1,0:T(8,128)S(1)} custom-call(s32[1,128]{1,0:T(1,128)} %bitcast.5, s32[1,128]{1,0:T(1,128)} %chosen_in.1, f32[3,256,1,128]{3,2,1,0:T(1,128)} %bitcast.3, s32[256,1,128]{2,1,0:T(1,128)} %bitcast.4, f32[3,32768]{1,0:T(4,128)} %tp_in.1, f32[3,32768]{1,0:T(4,128)} %tn_in.1), custom_call_target="tpu_custom_call" | custom-call | tf_op jit(solution)/shard_map/main/pallas_call | solution.py:409
  33.7 0.6 %copy.8 = f32[6,64]{1,0:T(8,128)} copy(f32[6,64]{1,0:T(8,128)S(1)} %main.1) | data formatting | bytes 3072

commit v7 on v5

--- a/solution.py
+++ b/solution.py
@@ -66,14 +66,17 @@
 
 def send_at(j, me, tiles):
     half, quarter = tiles // 2, tiles // 4
-    i = jnp.where(j <= quarter, j - 1, jnp.where(j <= half + quarter, quarter + (j - quarter - 1) // 2, 0))
-    n = jnp.where(j <= half + quarter, (j - quarter) // 2, j - half)
     place = me // quarter
     inner = (place // 2 + place) % 2
+    first = 6
+    mixed = j - first
+    is_far = (mixed <= 0) | ((mixed <= 2 * (half - first)) & (mixed % 2 == 1))
+    i = jnp.where(mixed <= 0, jnp.maximum(j - 1, 0), first + (mixed - 1) // 2)
+    n = jnp.where(mixed <= 2 * (half - first), mixed // 2, j - half)
     code = 3 - (inner * (1 - i // quarter) + (1 - inner) * (i % 2))
     low = inner * (i % quarter) + (1 - inner) * (i // 2)
     far = code * quarter + quarter - 1 - low
-    return flip(me, jnp.where((j <= quarter) | ((j <= half + quarter) & ((j - quarter) % 2 == 1)), far, half - n), tiles)
+    return flip(me, jnp.where(is_far, far, half - n), tiles)
 
 
 def recv_at(j, me, tiles):

time: 34.9 us -> 34.9 us (level)
  no operation moved by 1% of the time
where the time goes in v7:
time: 34.9 us; the launch traced here: 34.6 us
  Pallas kernels  34 us (97%)
  local copies, waits for them, and re-layouts  0.6 us (2%)
    pallas_call x1, Pallas kernels, body(): pl.pallas_call(main_kernel, out_shape=pltpu.VMEM((6, SCANS_DEV), f32), in...  34 us

profile of v7, /device:TPU:0, one launch (start us, length us, event | category | flops | bytes accessed | tf_op | source)
XLA Modules:
  0.0 34.6 jit_solution(2987340303184975375)
XLA Ops:
  0.0 34.0 %main.1 = f32[6,64]{1,0:T(8,128)S(1)} custom-call(s32[1,128]{1,0:T(1,128)} %bitcast.5, s32[1,128]{1,0:T(1,128)} %chosen_in.1, f32[3,256,1,128]{3,2,1,0:T(1,128)} %bitcast.3, s32[256,1,128]{2,1,0:T(1,128)} %bitcast.4, f32[3,32768]{1,0:T(4,128)} %tp_in.1, f32[3,32768]{1,0:T(4,128)} %tn_in.1), custom_call_target="tpu_custom_call" | custom-call | tf_op jit(solution)/shard_map/main/pallas_call | solution.py:401
  34.0 0.6 %copy.8 = f32[6,64]{1,0:T(8,128)} copy(f32[6,64]{1,0:T(8,128)S(1)} %main.1) | data formatting | bytes 3072
